TPU v7x, 256 devices: a whole 4x4x8 slice. The times are simulated.
256 devices in a mesh: img: 8 (over y, x_lo), cls: 8 (over z), emb: 4 (over x_hi, core).
Axes of the slice: x: 4 (x_hi: 2, x_lo: 2; x = x_hi * 2 + x_lo), y: 4, z: 8, core: 2. Of those that a mesh axis runs over, the one named last changes fastest.
Arguments:
- regions: bfloat16 [8192, 1024], P('img', 'emb'), may hold values from -8 to 8
- table: bfloat16 [21504, 1024], P('cls', 'emb'), may hold values from -1 to 1
- shift: float32 [8192], P('img'), may hold values from -0.5 to 0.1
- scale: float32 [8192], P('img'), may hold values from 2 to 20
- labels: int32 [8192], P('img'), may hold values from -1 to 21503, as said below
- valid: int32 [16, 21504], P('img', 'cls'), may hold values 0 or 1
Outputs:
- loss: float32 [], replicated
- region_grad: bfloat16 [8192, 1024], P('img', 'emb')
- table_grad: bfloat16 [21504, 1024], P('cls', 'emb')
Inputs may be any that keep to these rules, and one draw needn't show every extreme that they name: `labels`: -1 marks background; the first region of every image is foreground.
All inputs are finite; a program needn't handle non-finite values. No bound on the sum of `valid` on one device may be relied on, other than what follows from the above.
Results may differ from a plain program's by a relative error of at most 0.0034.
Values may be sent and summed in bfloat16 or wider, within the bound.
No kernel may reach another device: no remote copies, remote signals or barrier semaphores. Data moves between devices by JAX's collectives and lax.ppermute only.
A program may use at most 64 MiB of HBM per device.

v0:
```python
import functools
import jax
import jax.numpy as jnp
from jax import lax
from jax.sharding import Mesh
from jax.sharding import PartitionSpec as P

CLASSES = 21504
REG_IMG = 512
EMB = ("emb_0", "emb_1")
IMG = ("img_0", "img_1")
IMG_CLS_EMB = ("img_0", "img_1", "cls", "emb_0", "emb_1")


def over_axes(shard, axes):
    return functools.reduce(lax.psum, axes, shard)


def focal(logit, target):
    prob = jax.nn.sigmoid(logit)
    return -0.25 * target * (1.0 - prob) ** 2 * jax.nn.log_sigmoid(logit) - 0.75 * (
        1.0 - target
    ) * prob**2 * jax.nn.log_sigmoid(-logit)


def shards(regions, table, shift, scale, labels, valid):
    rows = regions.shape[0]
    class_dev = table.shape[0]
    parts = lax.axis_size(EMB)
    quarter = rows // parts
    start = lax.axis_index(EMB) * quarter
    block = regions.astype(jnp.float32)
    squares = lax.psum(jnp.sum(block * block, axis=1), EMB)
    local_count = jnp.sum((labels >= 0).astype(jnp.float32))
    count = lax.psum(local_count, IMG)
    inv = lax.rsqrt(squares + 1e-06)
    unit = block * inv[:, None]
    unit_b = unit.astype(jnp.bfloat16)
    unit_rows = lax.all_to_all(unit_b, EMB, split_axis=0, concat_axis=1, tiled=True)
    cosine = lax.dot_general(
        unit_rows,
        lax.all_gather(table, EMB, axis=1, tiled=True),
        (((1,), (1,)), ((), ())),
        preferred_element_type=jnp.float32,
    )
    shift_q = lax.dynamic_slice_in_dim(shift, start, quarter, 0)
    scale_q = lax.dynamic_slice_in_dim(scale, start, quarter, 0)
    label_q = lax.dynamic_slice_in_dim(labels, start, quarter, 0)
    image_ids = (start + jnp.arange(quarter, dtype=jnp.int32)) // REG_IMG
    onehot = (image_ids[:, None] == jnp.arange(valid.shape[0], dtype=jnp.int32)[None, :]).astype(
        jnp.float32
    )
    mask = jnp.dot(onehot, valid.astype(jnp.float32), preferred_element_type=jnp.float32)
    class_ids = lax.axis_index("cls") * class_dev + jnp.arange(class_dev, dtype=jnp.int32)
    logit = (cosine + shift_q[:, None]) * scale_q[:, None]
    target = (label_q[:, None] == class_ids[None, :]).astype(jnp.float32)
    term, pullback = jax.vjp(lambda value: focal(value, target), logit)
    dlogit = pullback(jnp.ones_like(term))[0]
    total = over_axes(jnp.sum(term * mask), IMG_CLS_EMB)
    factor = rows * lax.axis_size(IMG) / count
    dscore = (dlogit * mask * scale_q[:, None] * factor).astype(jnp.bfloat16)
    piece = lax.all_gather(dscore, EMB, axis=0, tiled=True)
    dunit_piece = jnp.dot(piece, table, preferred_element_type=jnp.float32)
    table_acc = lax.dot_general(
        piece, unit_b, (((0,), (0,)), ((), ())), preferred_element_type=jnp.float32
    )
    dunit = lax.psum(dunit_piece, "cls")
    radial = lax.psum(jnp.sum(unit * dunit, axis=1), EMB)
    region_grad = (inv[:, None] * (dunit - unit * radial[:, None])).astype(jnp.bfloat16)
    table_grad = lax.psum(table_acc, IMG).astype(jnp.bfloat16)
    loss = total / count / CLASSES
    return (loss, region_grad, table_grad)


def solution(mesh):
    torus = Mesh(
        mesh.devices.reshape(4, 2, mesh.shape["cls"], 2, 2),
        ("img_0", "img_1", "cls", "emb_0", "emb_1"),
    )
    return jax.shard_map(
        shards,
        mesh=torus,
        in_specs=(P(IMG, EMB), P("cls", EMB), P(IMG), P(IMG), P(IMG), P(IMG, "cls")),
        out_specs=(P(), P(IMG, EMB), P("cls", EMB)),
        check_vma=False,
    )
```

profile of v0, /device:TPU:1, one launch (start us, length us, event | category | flops | bytes accessed | tf_op | source)
XLA Modules:
  0.0 273.6 jit_solution(13197794882755454692)
XLA Ops:
  7.2 0.0 copy-start.2
  7.2 0.0 all-gather.3.cloned.1.call-start
  7.2 0.7 all-gather.3.cloned.1.call-update
  7.9 1.3 fusion.33
  9.2 9.7 %psum.70 = f32[1024]{0:T(1024)S(1)} all-reduce(f32[1024]{0:T(1024)S(1)} %fusion.33), channel_id=1, replica_groups=mesh['img_0'=4,'img_1'=2,'cls'=8,'emb_0'=2,'emb_1'=2] {'emb_0','emb_1'}, use_global_device_ids=true, to_apply=%region_1.0 | all-reduce | flops 1024 | bytes 8192 | tf_op jit(solution)/shard_map/psum | solution.py:33
  18.9 1.2 fusion.28
  20.2 1.0 copy.9
  21.2 5.2 %all-to-all-start = ((bf16[4,256,256]{1,2,0:T(8,128)(2,1)}), bf16[4,256,256]{1,2,0:T(8,128)(2,1)S(1)}, u32[]{:S(2)}, u32[]{:S(2)}) async-start(bf16[4,256,256]{1,2,0:T(8,128)(2,1)} %copy.9), calls=%async_computation | async-start | bytes 1048576 | tf_op jit(solution)/shard_map/all_to_all | solution.py:39
  26.3 0.0 all-gather.5.cloned.1.call-start
  26.3 0.0 copy-done.2
  26.3 0.6 convert_reduce_fusion
  26.9 24.0 %psum.76 = f32[]{:T(128)} all-reduce(f32[]{:T(128)} %convert_reduce_fusion), channel_id=1, replica_groups=mesh['img_0'=4,'img_1'=2,'cls'=8,'emb_0'=2,'emb_1'=2] {'img_0','img_1'}, use_global_device_ids=true, to_apply=%region_9.11 | all-reduce | flops 1 | bytes 8 | tf_op jit(solution)/shard_map/psum | solution.py:35
  51.0 0.1 dynamic_slice.9
  51.0 0.8 dynamic_slice.11
  51.8 0.8 dynamic_slice.10
  53.3 0.0 all-to-all-done
  53.3 15.6 %all-gather.3.cloned.1.call-done = bf16[2688,1024]{1,0:T(8,128)(2,1)} async-done(((bf16[2688,256]{1,0:T(8,128)(2,1)}), bf16[2688,1024]{1,0:T(8,128)(2,1)}) %all-gather.3.cloned.1.call-update) | async-done | bytes 5505040 | tf_op jit(solution)/shard_map/all_gather | solution.py:42
  68.9 0.0 copy-start.3
  68.9 4.5 %fusion = f32[256,2688]{1,0:T(8,128)S(1)} fusion(bf16[256,1024]{0,1:T(8,128)(2,1)S(1)} %bitcast.11, bf16[2688,1024]{1,0:T(8,128)(2,1)} %all-gather.3.cloned.1.call-done, f32[256]{0:T(256)S(1)} %dynamic_slice.11, f32[256]{0:T(256)S(1)} %dynamic_slice.10), kind=kOutput, calls=%fused_computation.7 | convolution fusion | flops 1410662400 | bytes 8783872 | tf_op jit(solution)/shard_map/dot_general | solution.py:40
  73.4 0.0 copy-done.3
  73.4 0.0 copy-start.1
  73.4 9.8 %fusion.12 = (bf16[256,2688]{1,0:T(8,128)(2,1)}, f32[]{:T(128)}) fusion(f32[256,2688]{1,0:T(8,128)S(1)} %fusion, f32[]{:T(128)S(6)} %div.31, f32[256]{0:T(256)S(1)} %dynamic_slice.11, s32[2688]{0:T(1024)S(1)} %iota_add_fusion, s32[256]{0:T(256)S(1)} %dynamic_slice.9, s32[2,2688]{1,0:T(2,128)S(1)} %copy-done.3, s32[256]{0:T(256)S(1)} %and_select_fusion), kind=kOutput, calls=%fused_computation.25 | convolution fusion | flops 47486720 | bytes 4164104 | tf_op jit(solution)/shard_map/dot_general | solution.py:53
  83.2 0.0 all-gather.5.cloned.1.call-update
  83.3 0.0 all-reduce.3.cloned.1.call-start
  83.3 9.4 %psum.71 = f32[]{:T(128)} all-reduce(f32[]{:T(128)} %get-tuple-element.12), channel_id=1, replica_groups=mesh['img_0'=4,'img_1'=2,'cls'=8,'emb_0'=2,'emb_1'=2] {'img_0'}, use_global_device_ids=true, to_apply=%region_3.5 | all-reduce | flops 1 | bytes 8 | tf_op jit(solution)/shard_map/psum | solution.py:16
  92.7 4.4 %psum.72 = f32[]{:T(128)} all-reduce(f32[]{:T(128)} %psum.71), channel_id=1, replica_groups=mesh['img_0'=4,'img_1'=2,'cls'=8,'emb_0'=2,'emb_1'=2] {'img_1'}, use_global_device_ids=true, to_apply=%region_4.6 | all-reduce | flops 1 | bytes 8 | tf_op jit(solution)/shard_map/psum | solution.py:16
  97.1 16.2 %psum.73 = f32[]{:T(128)} all-reduce(f32[]{:T(128)} %psum.72), channel_id=1, replica_groups=mesh['img_0'=4,'img_1'=2,'cls'=8,'emb_0'=2,'emb_1'=2] {'cls'}, use_global_device_ids=true, to_apply=%region_5.7 | all-reduce | flops 1 | bytes 8 | tf_op jit(solution)/shard_map/psum | solution.py:16
  113.3 6.5 %psum.74 = f32[]{:T(128)} all-reduce(f32[]{:T(128)} %psum.73), channel_id=1, replica_groups=mesh['img_0'=4,'img_1'=2,'cls'=8,'emb_0'=2,'emb_1'=2] {'emb_0'}, use_global_device_ids=true, to_apply=%region_6.8 | all-reduce | flops 1 | bytes 8 | tf_op jit(solution)/shard_map/psum | solution.py:16
  119.8 9.1 %psum.75 = f32[]{:T(128)} all-reduce(f32[]{:T(128)} %psum.74), channel_id=1, replica_groups=mesh['img_0'=4,'img_1'=2,'cls'=8,'emb_0'=2,'emb_1'=2] {'emb_1'}, use_global_device_ids=true, to_apply=%region_7.9 | all-reduce | flops 1 | bytes 8 | tf_op jit(solution)/shard_map/psum | solution.py:16
  130.2 1.8 all-gather.5.cloned.1.call-done
  132.0 0.0 copy-done.1
  132.0 5.2 %fusion.37 = f32[1024,256]{1,0:T(8,128)} fusion(bf16[1024,2688]{1,0:T(8,128)(2,1)} %all-gather.5.cloned.1.call-done, bf16[2688,256]{1,0:T(8,128)(2,1)S(1)} %copy-done.1), kind=kOutput, calls=%fused_computation.63 | convolution fusion | flops 1409286144 | bytes 7929856 | tf_op jit(solution)/shard_map/dot_general | solution.py:63
  137.2 0.0 all-reduce.3.cloned.1.call-update
  137.3 4.2 %fusion.38 = f32[2688,256]{1,0:T(8,128)S(1)} fusion(bf16[1024,2688]{1,0:T(8,128)(2,1)} %all-gather.5.cloned.1.call-done, bf16[1024,256]{1,0:T(8,128)(2,1)S(1)} %fusion.28), kind=kOutput, calls=%fused_computation.64 | convolution fusion | flops 1409286144 | bytes 8781824 | tf_op jit(solution)/shard_map/dot_general | solution.py:64
  141.5 0.0 copy-start
  141.5 111.4 %all-reduce.4 = bf16[2688,256]{1,0:T(8,128)(2,1)} all-reduce(f32[2688,256]{1,0:T(8,128)S(1)} %fusion.38), channel_id=1, replica_groups=mesh['img_0'=4,'img_1'=2,'cls'=8,'emb_0'=2,'emb_1'=2] {'img_0','img_1'}, use_global_device_ids=true, to_apply=%region_13.15 | all-reduce | flops 688128 | bytes 4128768 | tf_op jit(solution)/shard_map/psum | solution.py:70
  253.0 0.0 all-reduce.3.cloned.1.call-done
  253.0 0.0 copy-done
  253.0 1.6 fusion.29
  254.6 9.0 %psum.78 = f32[1024]{0:T(1024)S(1)} all-reduce(f32[1024]{0:T(1024)S(1)} %fusion.29), channel_id=1, replica_groups=mesh['img_0'=4,'img_1'=2,'cls'=8,'emb_0'=2,'emb_1'=2] {'emb_0','emb_1'}, use_global_device_ids=true, to_apply=%region_12.14 | all-reduce | flops 1024 | bytes 8192 | tf_op jit(solution)/shard_map/psum | solution.py:68
  263.5 2.4 fusion.32
  (3 shorter events, 0.0 us)
Async XLA Ops:
  7.2 19.2 %copy-start.2 = (s32[1024]{0:T(1024)S(1)}, s32[1024]{0:T(1024)}, u32[]{:S(2)}) copy-start(s32[1024]{0:T(1024)} %param.11) | copy-start | bytes 12292
  7.2 61.7 %all-gather.3.cloned.1.call-start = ((), (), s32[]{:S(2)}) async-start(), calls=%async_computation.1 | async-start | bytes 6881280 | tf_op jit(solution)/shard_map/all_gather | solution.py:42
  21.2 32.1 %all-to-all-start = ((bf16[4,256,256]{1,2,0:T(8,128)(2,1)}), bf16[4,256,256]{1,2,0:T(8,128)(2,1)S(1)}, u32[]{:S(2)}, u32[]{:S(2)}) async-start(bf16[4,256,256]{1,2,0:T(8,128)(2,1)} %copy.9), calls=%async_computation | async-start | bytes 1048576 | tf_op jit(solution)/shard_map/all_to_all | solution.py:39
  26.3 105.7 %all-gather.5.cloned.1.call-start = ((), (), s32[]{:S(2)}) async-start(), calls=%async_computation.2 | async-start | bytes 6881280 | tf_op jit(solution)/shard_map/all_gather | solution.py:62
  68.9 4.5 %copy-start.3 = (s32[2,2688]{1,0:T(2,128)S(1)}, s32[2,2688]{1,0:T(2,128)}, u32[]{:S(2)}) copy-start(s32[2,2688]{1,0:T(2,128)} %param.12) | copy-start | bytes 64516
  73.4 58.6 %copy-start.1 = (bf16[2688,256]{1,0:T(8,128)(2,1)S(1)}, bf16[2688,256]{1,0:T(8,128)(2,1)}, u32[]{:S(2)}) copy-start(bf16[2688,256]{1,0:T(8,128)(2,1)} %param.8) | copy-start | bytes 4128772
  83.3 169.7 %all-reduce.3.cloned.1.call-start = ((), (), s32[]{:S(2)}) async-start(), calls=%async_computation.3 | async-start | bytes 2097152 | tf_op jit(solution)/shard_map/psum | solution.py:67
  141.5 111.5 %copy-start = (bf16[1024,256]{1,0:T(8,128)(2,1)S(1)}, bf16[1024,256]{1,0:T(8,128)(2,1)}, u32[]{:S(2)}) copy-start(bf16[1024,256]{1,0:T(8,128)(2,1)} %param.7) | copy-start | bytes 1572868
Sparse Core Ops, SparseCore 0:
  9.8 59.0 all-gather.2
  83.4 48.5 all-gather.4
  137.4 70.8 all-reduce.2
where the time goes:
time: 274 us
  blocking collectives  200 us (73%)
  matrix products  23.8 us (9%)
  waiting for transfers between devices  18.1 us (7%)
  between operations  17 us (6%)
  other arithmetic  7.09 us (3%)
  starting transfers between devices  5.23 us (2%)
    psum x1, blocking collectives, shards(): table_grad = lax.psum(table_acc, IMG).astype(jnp.bfloat16)  111 us
    psum x5, blocking collectives, over_axes(): return functools.reduce(lax.psum, axes, shard)  45.6 us
    psum x1, blocking collectives, shards(): count = lax.psum(local_count, IMG)  24 us
    all_gather x1, waiting for transfers between devices, shards(): lax.all_gather(table, EMB, axis=1, tiled=True)  15.6 us
    dot_general x1, matrix products, shards(): jnp.dot(onehot, valid.astype(jnp.float32), preferred_element_type=jnp.flo...  9.78 us
    psum x1, blocking collectives, shards(): squares = lax.psum(jnp.sum(block * block, axis=1), EMB)  9.73 us
    psum x1, blocking collectives, shards(): radial = lax.psum(jnp.sum(unit * dunit, axis=1), EMB)  8.96 us
  transfers between devices with their start and end apart: 4, of which 2 were waited for; matrix products, arithmetic and copies ran while one was open for 4% of the time, Pallas kernels for 0%

commit v1 on v0

--- a/solution.py
+++ b/solution.py
@@ -67,7 +67,7 @@
     dunit = lax.psum(dunit_piece, "cls")
     radial = lax.psum(jnp.sum(unit * dunit, axis=1), EMB)
     region_grad = (inv[:, None] * (dunit - unit * radial[:, None])).astype(jnp.bfloat16)
-    table_grad = lax.psum(table_acc, IMG).astype(jnp.bfloat16)
+    table_grad = lax.psum(lax.psum(table_acc, "img_0"), "img_1").astype(jnp.bfloat16)
     loss = total / count / CLASSES
     return (loss, region_grad, table_grad)
 

time: 274 us -> 400 us (1.46)
  waiting for transfers between devices: 18.1 us -> 196 us
  blocking collectives: 200 us -> 146 us
    psum x1 -> x0, blocking collectives: 111 us -> none  [shards(): table_grad = lax.psum(table_acc, IMG).astype(jnp.bfloat16)]
    psum x1, waiting for transfers between devices: 0.01 us -> 74.4 us  [shards(): dunit = lax.psum(dunit_piece, 'cls')]
    psum x0 -> x1, waiting for transfers between devices: none -> 56.9 us  [shards(): lax.psum(table_acc, 'img_0')]
    psum x5, blocking collectives: 45.6 us -> 94.6 us  [over_axes(): return functools.reduce(lax.psum, axes, shard)]
    all_gather x1, waiting for transfers between devices: 1.81 us -> 48.6 us  [shards(): piece = lax.all_gather(dscore, EMB, axis=0, tiled=True)]
    psum x1, blocking collectives: 8.96 us -> 17.2 us  [shards(): radial = lax.psum(jnp.sum(unit * dunit, axis=1), EMB)]
  transfers between devices with their start and end apart: 4 -> 5, of which waited for: 2 -> 4; matrix products, arithmetic and copies ran while one was open for 4% -> 3% of each run, Pallas kernels for 0% -> 0%
where the time goes in v1:
time: 400 us; the launch traced here: 399 us
  waiting for transfers between devices  196 us (49%)
  blocking collectives  146 us (36%)
  matrix products  25.3 us (6%)
  between operations  17 us (4%)
  other arithmetic  5.95 us (1%)
  starting transfers between devices  5.28 us (1%)
    psum x5, blocking collectives, over_axes(): return functools.reduce(lax.psum, axes, shard)  94.6 us
    psum x1, waiting for transfers between devices, shards(): dunit = lax.psum(dunit_piece, 'cls')  74.4 us
    psum x1, waiting for transfers between devices, shards(): lax.psum(table_acc, 'img_0')  56.9 us
    all_gather x1, waiting for transfers between devices, shards(): piece = lax.all_gather(dscore, EMB, axis=0, tiled=True)  48.6 us
    psum x1, blocking collectives, shards(): count = lax.psum(local_count, IMG)  24 us
    psum x1, blocking collectives, shards(): radial = lax.psum(jnp.sum(unit * dunit, axis=1), EMB)  17.2 us
    all_gather x1, waiting for transfers between devices, shards(): lax.all_gather(table, EMB, axis=1, tiled=True)  15.6 us
    dot_general x1, matrix products, shards(): jnp.dot(onehot, valid.astype(jnp.float32), preferred_element_type=jnp.flo...  9.79 us
  transfers between devices with their start and end apart: 5, of which 4 were waited for; matrix products, arithmetic and copies ran while one was open for 3% of the time, Pallas kernels for 0%

profile of v1, /device:TPU:1, one launch (start us, length us, event | category | flops | bytes accessed | tf_op | source)
XLA Modules:
  0.0 399.3 jit_solution(11736235036073792527)
XLA Ops:
  7.2 0.0 copy-start.3
  7.2 0.0 all-gather.3.cloned.1.call-start
  7.2 0.7 all-gather.3.cloned.1.call-update
  7.9 1.3 fusion.33
  9.2 9.7 %psum.77 = f32[1024]{0:T(1024)S(1)} all-reduce(f32[1024]{0:T(1024)S(1)} %fusion.33), channel_id=1, replica_groups=mesh['img_0'=4,'img_1'=2,'cls'=8,'emb_0'=2,'emb_1'=2] {'emb_0','emb_1'}, use_global_device_ids=true, to_apply=%region_1.0 | all-reduce | flops 1024 | bytes 8192 | tf_op jit(solution)/shard_map/psum | solution.py:33
  18.9 1.2 fusion.28
  20.2 1.0 copy.9
  21.2 5.2 %all-to-all-start = ((bf16[4,256,256]{1,2,0:T(8,128)(2,1)}), bf16[4,256,256]{1,2,0:T(8,128)(2,1)S(1)}, u32[]{:S(2)}, u32[]{:S(2)}) async-start(bf16[4,256,256]{1,2,0:T(8,128)(2,1)} %copy.9), calls=%async_computation | async-start | bytes 1048576 | tf_op jit(solution)/shard_map/all_to_all | solution.py:39
  26.3 0.0 all-gather.5.cloned.1.call-start
  26.3 0.0 copy-done.3
  26.3 0.6 convert_reduce_fusion
  26.9 24.0 %psum.83 = f32[]{:T(128)} all-reduce(f32[]{:T(128)} %convert_reduce_fusion), channel_id=1, replica_groups=mesh['img_0'=4,'img_1'=2,'cls'=8,'emb_0'=2,'emb_1'=2] {'img_0','img_1'}, use_global_device_ids=true, to_apply=%region_9.11 | all-reduce | flops 1 | bytes 8 | tf_op jit(solution)/shard_map/psum | solution.py:35
  51.0 0.1 dynamic_slice.9
  51.0 0.8 dynamic_slice.11
  51.8 0.8 dynamic_slice.10
  53.3 0.0 all-to-all-done
  53.3 15.6 %all-gather.3.cloned.1.call-done = bf16[2688,1024]{1,0:T(8,128)(2,1)} async-done(((bf16[2688,256]{1,0:T(8,128)(2,1)}), bf16[2688,1024]{1,0:T(8,128)(2,1)}) %all-gather.3.cloned.1.call-update) | async-done | bytes 5505040 | tf_op jit(solution)/shard_map/all_gather | solution.py:42
  68.9 0.0 copy-start.4
  68.9 4.5 %fusion = f32[256,2688]{1,0:T(8,128)S(1)} fusion(bf16[256,1024]{0,1:T(8,128)(2,1)S(1)} %bitcast.11, bf16[2688,1024]{1,0:T(8,128)(2,1)} %all-gather.3.cloned.1.call-done, f32[256]{0:T(256)S(1)} %dynamic_slice.11, f32[256]{0:T(256)S(1)} %dynamic_slice.10), kind=kOutput, calls=%fused_computation.7 | convolution fusion | flops 1410662400 | bytes 8783872 | tf_op jit(solution)/shard_map/dot_general | solution.py:40
  73.4 0.0 copy-done.4
  73.4 9.8 %fusion.12 = (bf16[256,2688]{1,0:T(8,128)(2,1)}, f32[]{:T(128)}) fusion(f32[256,2688]{1,0:T(8,128)S(1)} %fusion, f32[]{:T(128)S(6)} %div.31, f32[256]{0:T(256)S(1)} %dynamic_slice.11, s32[2688]{0:T(1024)S(1)} %iota_add_fusion, s32[256]{0:T(256)S(1)} %dynamic_slice.9, s32[2,2688]{1,0:T(2,128)S(1)} %copy-done.4, s32[256]{0:T(256)S(1)} %and_select_fusion), kind=kOutput, calls=%fused_computation.25 | convolution fusion | flops 47486720 | bytes 4164104 | tf_op jit(solution)/shard_map/dot_general | solution.py:53
  83.2 0.0 all-gather.5.cloned.1.call-update
  83.2 0.0 all-reduce.7.cloned.1.call-start
  83.3 48.6 %all-gather.5.cloned.1.call-done = bf16[1024,2688]{1,0:T(8,128)(2,1)} async-done(((bf16[256,2688]{1,0:T(8,128)(2,1)}), bf16[1024,2688]{1,0:T(8,128)(2,1)}) %all-gather.5.cloned.1.call-update) | async-done | bytes 5505040 | tf_op jit(solution)/shard_map/all_gather | solution.py:62
  131.9 5.8 %fusion.38 = f32[2688,256]{1,0:T(8,128)} fusion(bf16[1024,2688]{1,0:T(8,128)(2,1)} %all-gather.5.cloned.1.call-done, bf16[1024,256]{1,0:T(8,128)(2,1)S(1)} %fusion.28), kind=kOutput, calls=%fused_computation.64 | convolution fusion | flops 1409286144 | bytes 8781824 | tf_op jit(solution)/shard_map/dot_general | solution.py:64
  137.7 0.0 copy-start.2
  137.7 0.0 all-reduce.7.cloned.1.call-update
  137.8 0.0 copy-start
  137.8 0.0 all-reduce.5.cloned.1.call-start
  137.8 1.3 copy-done.2
  139.1 5.2 %fusion.37 = f32[1024,256]{1,0:T(8,128)} fusion(bf16[1024,2688]{1,0:T(8,128)(2,1)} %all-gather.5.cloned.1.call-done, bf16[2688,256]{1,0:T(8,128)(2,1)S(1)} %copy-done.2), kind=kOutput, calls=%fused_computation.63 | convolution fusion | flops 1409286144 | bytes 7929856 | tf_op jit(solution)/shard_map/dot_general | solution.py:63
  144.3 0.0 all-reduce.5.cloned.1.call-update
  144.3 10.1 %psum.78 = f32[]{:T(128)} all-reduce(f32[]{:T(128)} %get-tuple-element.14), channel_id=1, replica_groups=mesh['img_0'=4,'img_1'=2,'cls'=8,'emb_0'=2,'emb_1'=2] {'img_0'}, use_global_device_ids=true, to_apply=%region_3.5 | all-reduce | flops 1 | bytes 8 | tf_op jit(solution)/shard_map/psum | solution.py:16
  154.4 56.9 %all-reduce.7.cloned.1.call-done = f32[2688,256]{1,0:T(8,128)} async-done(((f32[2688,256]{1,0:T(8,128)}), f32[2688,256]{1,0:T(8,128)}) %all-reduce.7.cloned.1.call-update) | async-done | bytes 2752528 | tf_op jit(solution)/shard_map/psum | solution.py:70
  211.3 74.4 %all-reduce.5.cloned.1.call-done = f32[1024,256]{1,0:T(8,128)} async-done(((f32[1024,256]{1,0:T(8,128)}), f32[1024,256]{1,0:T(8,128)}) %all-reduce.5.cloned.1.call-update) | async-done | bytes 1048592 | tf_op jit(solution)/shard_map/psum | solution.py:67
  285.7 0.0 copy-done
  285.7 0.0 copy-start.1
  285.7 1.7 fusion.29
  287.4 61.5 %all-reduce.8 = (f32[]{:T(128)}, bf16[2688,256]{1,0:T(8,128)(2,1)}) all-reduce(f32[]{:T(128)} %psum.78, f32[2688,256]{1,0:T(8,128)} %all-reduce.7.cloned.1.call-done), channel_id=1, replica_groups=mesh['img_0'=4,'img_1'=2,'cls'=8,'emb_0'=2,'emb_1'=2] {'img_1'}, use_global_device_ids=true, to_apply=%region_4.6 | all-reduce | flops 688129 | bytes 4128776 | tf_op jit(solution)/shard_map/psum | solution.py:16
  348.9 12.4 %psum.80 = f32[]{:T(128)} all-reduce(f32[]{:T(128)} %get-tuple-element.11), channel_id=1, replica_groups=mesh['img_0'=4,'img_1'=2,'cls'=8,'emb_0'=2,'emb_1'=2] {'cls'}, use_global_device_ids=true, to_apply=%region_5.7 | all-reduce | flops 1 | bytes 8 | tf_op jit(solution)/shard_map/psum | solution.py:16
  361.3 17.2 %psum.85 = f32[1024]{0:T(1024)S(1)} all-reduce(f32[1024]{0:T(1024)S(1)} %fusion.29), channel_id=1, replica_groups=mesh['img_0'=4,'img_1'=2,'cls'=8,'emb_0'=2,'emb_1'=2] {'emb_0','emb_1'}, use_global_device_ids=true, to_apply=%region_12.14 | all-reduce | flops 1024 | bytes 8192 | tf_op jit(solution)/shard_map/psum | solution.py:68
  378.6 6.0 %psum.81 = f32[]{:T(128)} all-reduce(f32[]{:T(128)} %psum.80), channel_id=1, replica_groups=mesh['img_0'=4,'img_1'=2,'cls'=8,'emb_0'=2,'emb_1'=2] {'emb_0'}, use_global_device_ids=true, to_apply=%region_6.8 | all-reduce | flops 1 | bytes 8 | tf_op jit(solution)/shard_map/psum | solution.py:16
  384.5 0.0 copy-done.1
  384.6 1.1 fusion.32
  385.7 4.6 %psum.82 = f32[]{:T(128)} all-reduce(f32[]{:T(128)} %psum.81), channel_id=1, replica_groups=mesh['img_0'=4,'img_1'=2,'cls'=8,'emb_0'=2,'emb_1'=2] {'emb_1'}, use_global_device_ids=true, to_apply=%region_7.9 | all-reduce | flops 1 | bytes 8 | tf_op jit(solution)/shard_map/psum | solution.py:16
  (3 shorter events, 0.0 us)
Async XLA Ops:
  7.2 19.2 %copy-start.3 = (s32[1024]{0:T(1024)S(1)}, s32[1024]{0:T(1024)}, u32[]{:S(2)}) copy-start(s32[1024]{0:T(1024)} %param.11) | copy-start | bytes 12292
  7.2 61.7 %all-gather.3.cloned.1.call-start = ((), (), s32[]{:S(2)}) async-start(), calls=%async_computation.1 | async-start | bytes 6881280 | tf_op jit(solution)/shard_map/all_gather | solution.py:42
  21.2 32.1 %all-to-all-start = ((bf16[4,256,256]{1,2,0:T(8,128)(2,1)}), bf16[4,256,256]{1,2,0:T(8,128)(2,1)S(1)}, u32[]{:S(2)}, u32[]{:S(2)}) async-start(bf16[4,256,256]{1,2,0:T(8,128)(2,1)} %copy.9), calls=%async_computation | async-start | bytes 1048576 | tf_op jit(solution)/shard_map/all_to_all | solution.py:39
  26.3 105.6 %all-gather.5.cloned.1.call-start = ((), (), s32[]{:S(2)}) async-start(), calls=%async_computation.2 | async-start | bytes 6881280 | tf_op jit(solution)/shard_map/all_gather | solution.py:62
  68.9 4.5 %copy-start.4 = (s32[2,2688]{1,0:T(2,128)S(1)}, s32[2,2688]{1,0:T(2,128)}, u32[]{:S(2)}) copy-start(s32[2,2688]{1,0:T(2,128)} %param.12) | copy-start | bytes 64516
  83.2 128.1 %all-reduce.7.cloned.1.call-start = ((), (), s32[]{:S(2)}) async-start(), calls=%async_computation.4 | async-start | bytes 5505024 | tf_op jit(solution)/shard_map/psum | solution.py:70
  137.7 1.3 copy-start.2
  137.8 147.9 %copy-start = (bf16[1024,256]{1,0:T(8,128)(2,1)S(1)}, bf16[1024,256]{1,0:T(8,128)(2,1)}, u32[]{:S(2)}) copy-start(bf16[1024,256]{1,0:T(8,128)(2,1)} %param.7) | copy-start | bytes 1572868
  137.8 147.9 %all-reduce.5.cloned.1.call-start = ((), (), s32[]{:S(2)}) async-start(), calls=%async_computation.3 | async-start | bytes 2097152 | tf_op jit(solution)/shard_map/psum | solution.py:67
  285.7 98.8 %copy-start.1 = (f32[1024,256]{1,0:T(8,128)S(1)}, f32[1024,256]{1,0:T(8,128)}, u32[]{:S(2)}) copy-start(f32[1024,256]{1,0:T(8,128)} %all-reduce.5.cloned.1.call-done) | copy-start | bytes 3145732
Sparse Core Ops, SparseCore 0:
  9.8 59.0 all-gather.2
  83.4 48.5 all-gather.4
  137.9 73.3 all-reduce.6
  214.1 71.5 all-reduce.4
